TPU v7x, 32 devices: a whole 2x2x4 slice. The times are simulated.
32 devices in a mesh: genome: 8 (over z, x), samples: 4 (over y, core).
Axes of the slice: x: 2, y: 2, z: 4, core: 2. Of those that a mesh axis runs over, the one named last changes fastest.
Arguments:
- genotypes: int32 [4096, 12288], P('samples', 'genome'), may hold values from 0 to 2
- residuals: bfloat16 [4096, 64], P('samples'), may hold values from -78 to 78
- variant_class: int32 [12288], P('genome'), may hold values from 0 to 7
- class_weight: float32 [8], replicated, may hold values from 0.25 to 4
- gene_start: int32 [512], P(('genome', 'samples')), may hold values from 0 to 12287, as said below
- gene_end: int32 [512], P(('genome', 'samples')), may hold values from 1 to 12288, as said below
Outputs:
- score_track: float32 [12288, 64], P(('genome', 'samples'))
- gene_stat: float32 [512, 64], P(('genome', 'samples'))
Inputs may be any that keep to these rules, and one draw needn't show every extreme that they name: gene_end[g] - 1 lies in [k * 384, (k + 1) * 384) with k = g // 16. 1 <= gene_end[g] - gene_start[g] <= 384.
All inputs are finite; a program needn't handle non-finite values.
Results may differ from a plain program's by a relative error of at most 0.0003.
Values sent between devices are 32-bit elements; how exact they have to be, the bound alone decides.
A program may use at most 64 MiB of HBM per device.

v0:
```python
import functools

import jax
import jax.numpy as jnp
from jax import lax
from jax.experimental import pallas as pl
from jax.experimental.pallas import tpu as pltpu
from jax.sharding import PartitionSpec as P

MESH = pl.DeviceIdType.MESH
GROUPS = 4
LANES = 128


def prefix(x, axis, combine, identity):
    peers, place = (lax.axis_size(axis), lax.axis_index(axis))
    everything = jax.tree.map(lambda part: lax.all_gather(part, axis), x)
    start = jax.tree.map(
        lambda part, zero: jnp.broadcast_to(jnp.asarray(zero, part.dtype), part.shape), x, identity
    )

    def step(k, before):
        reached = k < place
        new = combine(before, jax.tree.map(lambda part: part[k], everything))
        return jax.tree.map(lambda a, b: jnp.where(reached, a, b), new, before)

    return lax.fori_loop(0, peers, step, start)


def passed_along(value, axis, steps):
    count = lax.axis_size(axis)
    leading, last = (max(0, -steps), min(count, count - steps))
    return lax.ppermute(value, axis, [(source, source + steps) for source in range(leading, last)])


def add_pairs(earlier, later):
    return (earlier[0] + later[0], earlier[1] + later[1])


def prefix_rows(values):
    rows, columns = values.shape
    block_width = 128
    block_count = rows // block_width
    positions = jnp.arange(block_width)
    lower_ones = (positions[:, None] >= positions[None, :]).astype(jnp.float32)
    blocks = values.reshape(block_count, block_width, columns)
    inner_sums = jnp.einsum("ij,bjk->bik", lower_ones, blocks, precision=lax.Precision.HIGHEST)
    totals = inner_sums[:, -1, :]
    before = jnp.cumsum(totals, axis=0) - totals
    return (inner_sums + before[:, None, :]).reshape(rows, columns)


def local(genotypes, residuals, variant_class, class_weight, gene_start, gene_end):
    groups = lax.axis_size("samples")
    genome_count = lax.axis_size("genome")
    sample_rows, block_vars = genotypes.shape
    phenos = residuals.shape[1]
    share_rows = block_vars // groups
    total_samples = sample_rows * groups
    total_vars = block_vars * genome_count
    sample_part = lax.axis_index("samples")
    flat_index = lax.axis_index("genome") * groups + sample_part
    contract = (((0,), (0,)), ((), ()))
    dosage = genotypes.astype(jnp.bfloat16)
    partial_value = lax.dot_general(dosage, residuals, contract, preferred_element_type=jnp.float32)
    squared = lax.dot_general(
        dosage * dosage,
        jnp.ones((sample_rows,), jnp.bfloat16),
        contract,
        preferred_element_type=jnp.float32,
    )
    spread_local = jnp.sum(jnp.square(residuals.astype(jnp.float32)), axis=0)
    carry_zero = (jnp.zeros((phenos,), jnp.float32), jnp.zeros((), jnp.float32))
    summed, counts, spread_sum = lax.psum((partial_value, squared, spread_local), "samples")
    classes = jnp.arange(class_weight.shape[0], dtype=jnp.int32)
    weight = jnp.sum(
        jnp.where(variant_class[:, None] == classes[None, :], class_weight[None, :], 0.0), axis=1
    )
    scores = summed * weight[:, None] * total_samples ** (-0.5)
    quad_terms = weight * weight * counts / total_samples
    local_prefix = prefix_rows(scores)
    local_quad = prefix_rows(quad_terms[:, None])[:, 0]
    ends = (local_prefix[-1], local_quad[-1])
    carry_sum, carry_quad = prefix(ends, "genome", add_pairs, carry_zero)
    full_prefix = local_prefix + carry_sum[None, :]
    source, quad_source = (local_prefix, local_quad)
    last_rows = source[block_vars - share_rows :]
    last_quad = quad_source[block_vars - share_rows :]
    incoming, incoming_quad = passed_along((last_rows, last_quad), "genome", 1)
    incoming = incoming - incoming[-1][None, :]
    incoming_quad = incoming_quad - incoming_quad[-1]
    near_start = jnp.maximum(sample_part - 1, 0) * share_rows
    own_start = sample_part * share_rows
    near_rows = lax.dynamic_slice_in_dim(source, near_start, share_rows, 0)
    near_quad = lax.dynamic_slice_in_dim(quad_source, near_start, share_rows, 0)
    at_first = sample_part == 0
    prior_rows = jnp.where(at_first, incoming, near_rows)
    prior_quad = jnp.where(at_first, incoming_quad, near_quad)
    own_rows = lax.dynamic_slice_in_dim(source, own_start, share_rows, 0)
    own_quad = lax.dynamic_slice_in_dim(quad_source, own_start, share_rows, 0)
    track_rows = lax.dynamic_slice_in_dim(full_prefix, own_start, share_rows, 0)
    window = jnp.concatenate([prior_rows, own_rows], axis=0)
    quad_window = jnp.concatenate([prior_quad, own_quad], axis=0)
    window_base = (flat_index - 1) * share_rows
    positions = jnp.arange(2 * share_rows, dtype=jnp.int32)
    end_pos = gene_end - 1 - window_base
    start_pos = gene_start - 1 - window_base
    picker = (positions[None, :] == end_pos[:, None]).astype(jnp.float32) - (
        positions[None, :] == start_pos[:, None]
    ).astype(jnp.float32)
    gene_score = jnp.dot(
        picker, window, precision=lax.Precision.HIGHEST, preferred_element_type=jnp.float32
    )
    gene_quad = jnp.dot(
        picker, quad_window, precision=lax.Precision.HIGHEST, preferred_element_type=jnp.float32
    )
    variance = spread_sum / total_samples + 1e-05
    gene_stat = jnp.square(gene_score) / (variance[None, :] * (gene_quad[:, None] + 1.0))
    return (track_rows * total_vars ** (-0.5), gene_stat)


def split3(x):
    high = x.astype(jnp.bfloat16)
    rest = x - high.astype(jnp.float32)
    mid = rest.astype(jnp.bfloat16)
    low = (rest - mid.astype(jnp.float32)).astype(jnp.bfloat16)
    return jnp.concatenate([high, mid, low], axis=0)


def dot3(x, y):
    rows = x.shape[0]
    out = jnp.dot(split3(x), y, preferred_element_type=jnp.float32)
    return out[:rows] + out[rows : 2 * rows] + out[2 * rows :]


def kernel(
    genome_count, geno_hbm, res_hbm, class_hbm, cw_hbm, start_hbm, end_hbm,
    track_ref, stat_ref,
    res_ref, class_ref, cw_ref, bounds_ref, small_sem,
    geno, scores, relay, partials, bounds_in, gene_out, gene_in, tot_out, tot_in,
    geno_sem, rs_send, rs_recv, bd_send, bd_recv, bn_send, bn_recv,
    ge_send, ge_recv, gn_send, gn_recv, to_send, to_recv,
):
    g = lax.axis_index("genome")
    s = lax.axis_index("samples")
    sample_rows, share = geno.shape[1:]
    block = share * GROUPS
    phenos = res_ref.shape[0]
    genes = stat_ref.shape[0]
    depth = scores.shape[1]
    total_samples = sample_rows * GROUPS
    peers = [lax.rem(s + 2, 4), 3 - s, s + 1 - 2 * lax.rem(s, 2)]
    owners = peers + [s]

    barrier = pltpu.get_barrier_semaphore()
    for dg in range(genome_count):
        for ds in range(GROUPS):
            if dg or ds:
                there = (lax.rem(g + dg, genome_count), lax.rem(s + ds, GROUPS))
                pl.semaphore_signal(barrier, inc=1, device_id=there, device_id_type=MESH)

    smalls = []
    for i, (src, dst) in enumerate([
        (res_hbm, res_ref), (class_hbm, class_ref), (cw_hbm, cw_ref),
        (start_hbm, bounds_ref.at[0]), (end_hbm, bounds_ref.at[1]),
    ]):
        copy = pltpu.make_async_copy(src, dst, small_sem.at[i])
        copy.start()
        smalls.append(copy)
    loads = []
    for j, owner in enumerate(owners):
        columns = pl.ds(pl.multiple_of(owner * share, LANES), share)
        copy = pltpu.make_async_copy(geno_hbm.at[:, columns], geno.at[j], geno_sem.at[j])
        copy.start()
        loads.append(copy)

    def remote(src, dst, send, recv, there):
        return pltpu.make_async_remote_copy(
            src_ref=src, dst_ref=dst, send_sem=send, recv_sem=recv,
            device_id=there, device_id_type=MESH,
        )

    def chunk(j):
        loads[j].wait()
        acc = jnp.zeros((phenos, share), jnp.float32)
        squares = jnp.zeros((8, share), jnp.float32)
        step = 256
        for k in range(0, sample_rows, step):
            x = geno[j, k : k + step, :].astype(jnp.float32)
            squares = squares + jnp.sum((x * x).reshape(step // 8, 8, share), axis=0)
            acc = acc + jnp.dot(
                res_ref[:, k : k + step], x.astype(jnp.bfloat16),
                preferred_element_type=jnp.float32,
            )
        counts = jnp.sum(squares, axis=0, keepdims=True)
        rows = share // LANES
        kind = jnp.concatenate(
            [class_ref[pl.ds(owners[j] * rows + i, 1), :] for i in range(rows)], axis=1
        )
        weight = jnp.zeros((1, share), jnp.float32)
        for c in range(cw_ref.shape[0]):
            weight = jnp.where(kind == c, cw_ref[c], weight)
        scores[j, :phenos, :] = acc * (weight * total_samples ** (-0.5))
        quad = weight * weight * counts / total_samples
        first = lax.broadcasted_iota(jnp.int32, (depth - phenos, share), 0) == 0
        scores[j, phenos:, :] = jnp.where(first, quad, 0.0)

    def rs_copy(r):
        return remote(
            scores.at[r, pl.ds(0, phenos)], partials.at[r], rs_send.at[r], rs_recv.at[r],
            (g, peers[2]),
        )

    for copy in smalls:
        copy.wait()
    chunk(0)
    chunk(1)
    chunk(2)
    chunk(3)

    chunk_sums = [jnp.sum(scores[j], axis=1, keepdims=True) for j in range(GROUPS)]
    wide = lax.broadcasted_iota(jnp.int32, (LANES, LANES), 1)

    def tall(column):
        fill = jnp.zeros((LANES - column.shape[0], 1), jnp.float32)
        return jnp.concatenate([column, fill], axis=0)

    squared = jnp.square(res_ref[...].astype(jnp.float32))
    columns = [jnp.sum(squared, axis=1, keepdims=True)]
    for k in range(GROUPS + 1):
        total = jnp.zeros((depth, 1), jnp.float32)
        for j in range(GROUPS):
            total = total + jnp.where(owners[j] < k, chunk_sums[j], 0.0)
        columns.append(total)
    totals = jnp.zeros((LANES, LANES), jnp.float32)
    for i, column in enumerate(columns):
        totals = jnp.where(wide == i, tall(column), totals)
    totals = jnp.transpose(totals)
    tot_out[...] = totals[GROUPS + 1 : GROUPS + 2]
    pl.semaphore_wait(barrier, genome_count * GROUPS - 1)

    bound_copies = []
    for r in range(3):
        copy = remote(bounds_ref, bounds_in.at[s], bd_send.at[r], bd_recv.at[r], (g, peers[r]))
        copy.start()
        bound_copies.append(copy)
    sends_back = jnp.logical_and(s == 0, g > 0)
    has_next = g < genome_count - 1
    before = lax.rem(g + genome_count - 1, genome_count)
    after = lax.rem(g + 1, genome_count)
    back_copies = [
        remote(bounds_ref, bounds_in.at[GROUPS], bn_send.at[k], bn_recv, (before, k))
        for k in range(GROUPS)
    ]

    @pl.when(sends_back)
    def _():
        for copy in back_copies:
            copy.start()

    rs = [rs_copy(r) for r in (1, 2)]
    for copy in rs:
        copy.start()
    to_copies = []
    for dg in range(1, genome_count):
        for ds in range(GROUPS):
            k = (dg - 1) * GROUPS + ds
            there = (lax.rem(g + dg, genome_count), lax.rem(s + ds, GROUPS))
            to_copies.append(
                (dg, remote(tot_out, tot_in.at[k], to_send.at[k], to_recv.at[k], there))
            )
    for dg in range(genome_count - 1, 0, -1):

        @pl.when(g + dg < genome_count)
        def _(dg=dg):
            for d, copy in to_copies:
                if d == dg:
                    copy.start()

    rs[0].wait()
    relay[...] = scores[0, :phenos, :] + partials[1]
    across = remote(relay, partials.at[0], rs_send.at[0], rs_recv.at[0], (g, peers[0]))
    across.start()
    for copy in bound_copies:
        copy.wait()

    @pl.when(has_next)
    def _():
        back_copies[0].wait_recv()

    lane = lax.broadcasted_iota(jnp.int32, (1, LANES), 1)
    group_of = lane // genes
    start_row = jnp.zeros((1, LANES), jnp.int32)

    def tiled(row):
        return jnp.concatenate([row] * (LANES // genes), axis=1)

    own_bounds = (tiled(bounds_ref[0]), tiled(bounds_ref[1]))
    end_row = jnp.zeros((1, LANES), jnp.int32)
    base = g * block
    for k in range(GROUPS + 1):
        if k < GROUPS:
            use = group_of == k
            lows = jnp.where(s == k, own_bounds[0], tiled(bounds_in[k, 0]))
            tops = jnp.where(s == k, own_bounds[1], tiled(bounds_in[k, 1]))
        else:
            use = jnp.logical_and(group_of == k, has_next)
            lows = tiled(bounds_in[k, 0])
            tops = tiled(bounds_in[k, 1])
        start_row = jnp.where(use, lows - base, start_row)
        end_row = jnp.where(use, tops - base, end_row)

    sums = jnp.zeros((depth, LANES), jnp.float32)
    for j in range(GROUPS):
        v = lax.broadcasted_iota(jnp.int32, (share, LANES), 0) + owners[j] * share
        inside = jnp.logical_and(v >= start_row, v < end_row)
        picker = jnp.where(inside, 1.0, 0.0).astype(jnp.bfloat16)
        sums = sums + dot3(scores[j], picker)
    table = jnp.transpose(
        jnp.concatenate([sums, jnp.zeros((LANES - depth, LANES), jnp.float32)], axis=0)
    )
    for k in range(GROUPS + 1):
        gene_out[k, :genes, :] = table[k * genes : (k + 1) * genes]
        row = lax.broadcasted_iota(jnp.int32, (8, LANES), 0)
        gene_out[k, genes:, :] = jnp.where(
            row == 0, totals[:1], jnp.where(row == 1, totals[1 + k : 2 + k], 0.0)
        )
    ge_copies = []
    for r in range(3):
        copy = remote(
            gene_out.at[peers[r]], gene_in.at[r], ge_send.at[r], ge_recv.at[r], (g, peers[r])
        )
        copy.start()
        ge_copies.append(copy)
    next_copy = remote(
        gene_out.at[GROUPS], gene_in.at[3 + s], gn_send, gn_recv.at[s], (after, 0)
    )

    @pl.when(has_next)
    def _():
        next_copy.start()

    row_u = lax.broadcasted_iota(jnp.int32, (share, share), 0)
    col_v = lax.broadcasted_iota(jnp.int32, (share, share), 1)
    upper = jnp.where(row_u <= col_v, 1.0, 0.0).astype(jnp.bfloat16)
    rs[1].wait()
    across.wait()
    summed = (scores[3, :phenos, :] + partials[2]) + partials[0]
    prefix = dot3(summed, upper)

    for copy in ge_copies:
        copy.wait()
    mine = (gene_out[s] + gene_in[2]) + (gene_in[0] + gene_in[1])
    for k in range(GROUPS):
        arrival = remote(
            gene_out.at[GROUPS], gene_in.at[3 + k], gn_send, gn_recv.at[k], (before, k)
        )
        pl.when(sends_back)(arrival.wait_recv)
    extra = (gene_in[3] + gene_in[4]) + (gene_in[5] + gene_in[6])
    gene_rows = mine[:genes] + jnp.where(sends_back, extra[:genes], 0.0)
    variance = mine[genes : genes + 1, :phenos] / total_samples + 1e-05
    quad = gene_rows[:, phenos : phenos + 1]
    stat_ref[...] = jnp.square(gene_rows[:, :phenos]) / (variance * (quad + 1.0))

    carry = mine[genes + 1 : genes + 2]
    for dg in range(1, genome_count):

        @pl.when(g - dg >= 0)
        def _(dg=dg):
            for d, copy in to_copies:
                if d == dg:
                    copy.wait_recv()

        k = (dg - 1) * GROUPS
        four = (tot_in[k] + tot_in[k + 1]) + (tot_in[k + 2] + tot_in[k + 3])
        carry = carry + jnp.where(g - dg >= 0, four, 0.0)
    column = jnp.transpose(jnp.broadcast_to(carry, (LANES, LANES)))[:phenos]
    for k in range(0, share, LANES):
        track_ref[:, k : k + LANES] = prefix[:, k : k + LANES] + column

    for dg in range(1, genome_count):

        @pl.when(g + dg < genome_count)
        def _(dg=dg):
            for d, copy in to_copies:
                if d == dg:
                    copy.wait_send()

    pl.when(has_next)(next_copy.wait_send)

    @pl.when(sends_back)
    def _():
        for copy in back_copies:
            copy.wait_send()


def finish(scale, track_in, stat_in, track_out, stat_out):
    track_out[...] = track_in[...] * scale
    stat_out[...] = stat_in[...]


def local_kernel(genotypes, residuals, variant_class, class_weight, gene_start, gene_end):
    genome_count = lax.axis_size("genome")
    sample_rows, block_vars = genotypes.shape
    phenos = residuals.shape[1]
    share = block_vars // GROUPS
    genes = gene_start.shape[0]
    depth = phenos + 16
    far = (genome_count - 1) * GROUPS
    vmem = pl.BlockSpec(memory_space=pltpu.VMEM)
    dma = pltpu.SemaphoreType.DMA
    track, stat = pl.pallas_call(
        functools.partial(kernel, genome_count),
        out_shape=(
            jax.ShapeDtypeStruct((phenos, share), jnp.float32),
            jax.ShapeDtypeStruct((genes, phenos), jnp.float32),
        ),
        in_specs=[pl.BlockSpec(memory_space=pltpu.HBM)] * 6,
        out_specs=(vmem, vmem),
        scratch_shapes=[
            pltpu.VMEM((phenos, sample_rows), jnp.bfloat16),
            pltpu.VMEM((block_vars // LANES, LANES), jnp.int32),
            pltpu.SMEM(class_weight.shape, jnp.float32),
            pltpu.VMEM((2, 1, genes), jnp.int32),
            dma((5,)),
            pltpu.VMEM((GROUPS, sample_rows, share), jnp.int32),
            pltpu.VMEM((GROUPS, depth, share), jnp.float32),
            pltpu.VMEM((phenos, share), jnp.float32),
            pltpu.VMEM((3, phenos, share), jnp.float32),
            pltpu.VMEM((GROUPS + 1, 2, 1, genes), jnp.int32),
            pltpu.VMEM((GROUPS + 1, genes + 8, LANES), jnp.float32),
            pltpu.VMEM((3 + GROUPS, genes + 8, LANES), jnp.float32),
            pltpu.VMEM((1, LANES), jnp.float32),
            pltpu.VMEM((far, 1, LANES), jnp.float32),
            dma((GROUPS,)), dma((3,)), dma((3,)), dma((3,)), dma((3,)), dma((GROUPS,)), dma(()),
            dma((3,)), dma((3,)), dma(()), dma((GROUPS,)), dma((far,)), dma((far,)),
        ],
        compiler_params=pltpu.CompilerParams(
            collective_id=0, has_side_effects=True, vmem_limit_bytes=67043328
        ),
    )(
        genotypes, residuals.T, variant_class.reshape(block_vars // LANES, LANES), class_weight,
        gene_start.reshape(1, genes), gene_end.reshape(1, genes),
    )
    scale = (block_vars * genome_count) ** (-0.5)
    track, stat = pl.pallas_call(
        functools.partial(finish, scale),
        out_shape=(
            jax.ShapeDtypeStruct(track.shape, jnp.float32),
            jax.ShapeDtypeStruct(stat.shape, jnp.float32),
        ),
        in_specs=[vmem, vmem],
        out_specs=(vmem, vmem),
    )(track, stat)
    return track.T, stat


def solution(mesh):
    groups = mesh.shape["samples"]

    def body(genotypes, residuals, variant_class, class_weight, gene_start, gene_end):
        args = (genotypes, residuals, variant_class, class_weight, gene_start, gene_end)
        share = genotypes.shape[1] // groups
        genes = gene_start.shape[0]
        fits = LANES % genes == 0 and (GROUPS + 1) * genes <= LANES
        aligned = share % LANES == 0 and genotypes.shape[0] % 256 == 0 and genes % 8 == 0
        if groups == GROUPS and fits and aligned:
            return local_kernel(*args)
        return local(*args)

    return jax.shard_map(
        body,
        mesh=mesh,
        in_specs=(
            P("samples", "genome"),
            P("samples", None),
            P("genome"),
            P(),
            P(("genome", "samples")),
            P(("genome", "samples")),
        ),
        out_specs=(P(("genome", "samples"), None), P(("genome", "samples"), None)),
        check_vma=False,
    )
```

profile of v0, /device:TPU:0, one launch (start us, length us, event | category | flops | bytes accessed | tf_op | source)
XLA Modules:
  0.0 16.9 jit_solution(7515401617151699316)
XLA Ops:
  0.6 14.8 %shard_map.77 = (f32[64,384]{1,0:T(8,128)}, f32[16,64]{1,0:T(8,128)}) custom-call(s32[1024,1536]{1,0:T(8,128)} %geno_hbm.1, bf16[64,1024]{1,0:T(8,128)(2,1)} %bitcast.5, s32[12,128]{1,0:T(8,128)} %bitcast.6, f32[8]{0:T(128)} %cw_hbm.1, s32[1,16]{1,0:T(1,128)} %bitcast.7, s32[1,16]{1,0:T(1,128)} %bitcast.8), custom_call_target="tpu_custom_call" | custom-call | tf_op jit(solution)/shard_map/pallas_call | solution.py:412
  15.4 1.5 %shard_map.78 = (f32[64,384]{1,0:T(8,128)}, f32[16,64]{1,0:T(8,128)}) custom-call(f32[64,384]{1,0:T(8,128)} %get-tuple-element.6.track_in, f32[16,64]{1,0:T(8,128)} %get-tuple-element.7.stat_in), custom_call_target="tpu_custom_call" | custom-call | tf_op jit(solution)/shard_map/pallas_call | solution.py:446
where the time goes:
time: 17.1 us; the launch traced here: 16.9 us
  Pallas kernels  16.3 us (95%)
  between operations  0.64 us (4%)
    pallas_call x1, Pallas kernels, local_kernel(): pl.pallas_call(functools.partial(kernel, genome_count), out_shape=(jax.Sh...  14.8 us
    pallas_call x1, Pallas kernels, local_kernel(): pl.pallas_call(functools.partial(finish, scale), out_shape=(jax.ShapeDtyp...  1.55 us

commit v1 on v0

--- a/solution.py
+++ b/solution.py
@@ -10,6 +10,7 @@
 MESH = pl.DeviceIdType.MESH
 GROUPS = 4
 LANES = 128
+VMEM_LIMIT = 24 * 1024 * 1024
 
 
 def prefix(x, axis, combine, identity):
@@ -152,13 +153,6 @@
     peers = [lax.rem(s + 2, 4), 3 - s, s + 1 - 2 * lax.rem(s, 2)]
     owners = peers + [s]
 
-    barrier = pltpu.get_barrier_semaphore()
-    for dg in range(genome_count):
-        for ds in range(GROUPS):
-            if dg or ds:
-                there = (lax.rem(g + dg, genome_count), lax.rem(s + ds, GROUPS))
-                pl.semaphore_signal(barrier, inc=1, device_id=there, device_id_type=MESH)
-
     smalls = []
     for i, (src, dst) in enumerate([
         (res_hbm, res_ref), (class_hbm, class_ref), (cw_hbm, cw_ref),
@@ -173,6 +167,13 @@
         copy = pltpu.make_async_copy(geno_hbm.at[:, columns], geno.at[j], geno_sem.at[j])
         copy.start()
         loads.append(copy)
+
+    barrier = pltpu.get_barrier_semaphore()
+    for dg in range(genome_count):
+        for ds in range(GROUPS):
+            if dg or ds:
+                there = (lax.rem(g + dg, genome_count), lax.rem(s + ds, GROUPS))
+                pl.semaphore_signal(barrier, inc=1, device_id=there, device_id_type=MESH)
 
     def remote(src, dst, send, recv, there):
         return pltpu.make_async_remote_copy(
@@ -412,8 +413,8 @@
     track, stat = pl.pallas_call(
         functools.partial(kernel, genome_count),
         out_shape=(
-            jax.ShapeDtypeStruct((phenos, share), jnp.float32),
-            jax.ShapeDtypeStruct((genes, phenos), jnp.float32),
+            pltpu.VMEM((phenos, share), jnp.float32),
+            pltpu.VMEM((genes, phenos), jnp.float32),
         ),
         in_specs=[pl.BlockSpec(memory_space=pltpu.HBM)] * 6,
         out_specs=(vmem, vmem),
@@ -436,22 +437,28 @@
             dma((3,)), dma((3,)), dma(()), dma((GROUPS,)), dma((far,)), dma((far,)),
         ],
         compiler_params=pltpu.CompilerParams(
-            collective_id=0, has_side_effects=True, vmem_limit_bytes=67043328
+            collective_id=0, has_side_effects=True, vmem_limit_bytes=VMEM_LIMIT
         ),
-    )(
-        genotypes, residuals.T, variant_class.reshape(block_vars // LANES, LANES), class_weight,
-        gene_start.reshape(1, genes), gene_end.reshape(1, genes),
-    )
+    )(*(
+        pltpu.with_memory_space_constraint(a, pltpu.HBM)
+        for a in (
+            genotypes, residuals.T, variant_class.reshape(block_vars // LANES, LANES), class_weight,
+            gene_start.reshape(1, genes), gene_end.reshape(1, genes),
+        )
+    ))
     scale = (block_vars * genome_count) ** (-0.5)
     track, stat = pl.pallas_call(
         functools.partial(finish, scale),
         out_shape=(
-            jax.ShapeDtypeStruct(track.shape, jnp.float32),
-            jax.ShapeDtypeStruct(stat.shape, jnp.float32),
+            jax.ShapeDtypeStruct((phenos, share), jnp.float32),
+            jax.ShapeDtypeStruct((genes, phenos), jnp.float32),
         ),
         in_specs=[vmem, vmem],
         out_specs=(vmem, vmem),
-    )(track, stat)
+    )(
+        pltpu.with_memory_space_constraint(track, pltpu.VMEM),
+        pltpu.with_memory_space_constraint(stat, pltpu.VMEM),
+    )
     return track.T, stat
 
 

time: 17.1 us -> 15.6 us (0.912)
  Pallas kernels: 16.3 us -> 14.8 us
    pallas_call x1, Pallas kernels: 1.55 us -> 0.65 us  [local_kernel(): pl.pallas_call(functools.partial(finish, scale), out_shape=(jax.ShapeDtyp...]
    pallas_call x1, Pallas kernels: 14.8 us -> 14.1 us  [local_kernel(): pl.pallas_call(functools.partial(kernel, genome_count), out_shape=(pltpu....]
where the time goes in v1:
time: 15.6 us; the launch traced here: 15.4 us
  Pallas kernels  14.8 us (95%)
  between operations  0.64 us (4%)
    pallas_call x1, Pallas kernels, local_kernel(): pl.pallas_call(functools.partial(kernel, genome_count), out_shape=(pltpu....  14.1 us
    pallas_call x1, Pallas kernels, local_kernel(): pl.pallas_call(functools.partial(finish, scale), out_shape=(jax.ShapeDtyp...  0.65 us

profile of v1, /device:TPU:0, one launch (start us, length us, event | category | flops | bytes accessed | tf_op | source)
XLA Modules:
  0.0 15.4 jit_solution(18435578599988898151)
XLA Ops:
  0.6 14.1 %shard_map.77 = (f32[64,384]{1,0:T(8,128)S(1)}, f32[16,64]{1,0:T(8,128)S(1)}) custom-call(s32[1024,1536]{1,0:T(8,128)} %geno_hbm.1, bf16[64,1024]{1,0:T(8,128)(2,1)} %bitcast.5, s32[12,128]{1,0:T(8,128)} %bitcast.6, f32[8]{0:T(128)} %cw_hbm.1, s32[1,16]{1,0:T(1,128)} %bitcast.7, s32[1,16]{1,0:T(1,128)} %bitcast.8), custom_call_target="tpu_custom_call" | custom-call | tf_op jit(solution)/shard_map/pallas_call | solution.py:413
  14.8 0.7 %shard_map.78 = (f32[64,384]{1,0:T(8,128)}, f32[16,64]{1,0:T(8,128)}) custom-call(f32[64,384]{1,0:T(8,128)S(1)} %get-tuple-element.6.track_in, f32[16,64]{1,0:T(8,128)S(1)} %get-tuple-element.7.stat_in), custom_call_target="tpu_custom_call" | custom-call | tf_op jit(solution)/shard_map/pallas_call | solution.py:450
